TPU v7x, 8 devices: a whole 2x2x1 slice. The times are simulated.
8 devices in a mesh: row: 2 (over z, y), col: 4 (over x, core).
Axes of the slice: x: 2, y: 2, z: 1, core: 2. Of those that a mesh axis runs over, the one named last changes fastest.
Arguments:
- v_panels: float32 [4096, 4096], P('row', 'col')
- t_factors: float32 [64, 64, 64], P('col')
- z_vectors: float32 [4096, 2048], P(None, ('col', 'row'))
Outputs:
- output: float32 [4096, 2048], P('row', 'col')
All inputs are finite; a program needn't handle non-finite values.
Results may differ from a plain program's by a relative error of at most 0.001.
Values sent between devices are 32-bit elements.
A program may use at most 1 GiB of HBM per device.

v0:
```python
import jax
import jax.numpy as jnp
from jax import lax
from jax.sharding import PartitionSpec as P, NamedSharding

HIGHEST = lax.Precision.HIGHEST


def solution(mesh):
    col_devs = mesh.shape['col']

    def local_apply(v_loc, t_loc, z_loc):
        panel_width = t_loc.shape[1]
        groups = t_loc.shape[0]
        x_loc = lax.all_to_all(z_loc, 'row', 0, 1, tiled=True)

        def group_step(step_idx, x_cur):
            group_idx = groups - 1 - step_idx
            v_blk = lax.dynamic_slice_in_dim(v_loc, group_idx * panel_width, panel_width, axis=1)
            t_blk = lax.dynamic_index_in_dim(t_loc, group_idx, axis=0, keepdims=False)
            v_group = lax.all_gather(v_blk, 'col', axis=0)
            t_group = lax.all_gather(t_blk, 'col', axis=0)

            def panel_step(pos_idx, x_in):
                col_pos = col_devs - 1 - pos_idx
                v_j = lax.dynamic_index_in_dim(v_group, col_pos, axis=0, keepdims=False)
                t_j = lax.dynamic_index_in_dim(t_group, col_pos, axis=0, keepdims=False)
                w_part = jnp.einsum('na,nk->ak', v_j, x_in, precision=HIGHEST, preferred_element_type=jnp.float32)
                w_full = lax.psum(w_part, 'row')
                y_mat = jnp.dot(t_j, w_full, precision=HIGHEST, preferred_element_type=jnp.float32)
                return x_in - jnp.dot(v_j, y_mat, precision=HIGHEST, preferred_element_type=jnp.float32)

            return lax.fori_loop(0, col_devs, panel_step, x_cur)

        return lax.fori_loop(0, groups, group_step, x_loc)

    return jax.shard_map(local_apply, mesh=mesh,
                         in_specs=(P('row', 'col'), P('col', None, None), P(None, ('col', 'row'))),
                         out_specs=P('row', 'col'), check_vma=False)
```

profile of v0, /device:TPU:0, one launch (start us, length us, event | category | flops | bytes accessed | tf_op | source)
XLA Modules:
  0.0 2517.5 jit_solution(17555532736149065819)
XLA Ops:
  12.2 48.9 %all-to-all-done = f32[2,2048,256]{2,1,0:T(8,128)} async-done(((f32[2,2048,256]{2,1,0:T(8,128)}), f32[2,2048,256]{2,1,0:T(8,128)}, u32[]{:S(2)}, u32[]{:S(2)}) %all-to-all-start) | async-done | bytes 4194336 | tf_op jit(solution)/shard_map/all_to_all | solution.py:15
  71.9 2438.8 %while.44 = (s32[]{:T(128)}, f32[2048,512]{1,0:T(8,128)}, f32[2048,1024]{1,0:T(8,128)}, f32[16,64,64]{2,1,0:T(8,128)}, s32[]{:T(128)}, /*index=5*/s32[]{:T(128)}...) while((s32[]{:T(128)}, f32[2048,512]{1,0:T(8,128)}, ...), condition=%wide.region_4.5_spmd, body=%wide.region_0.4_spmd.sunk | while | flops 1636859904 | bytes 27673112 | solution.py:35
  106.7 117.8 %while.45 = (s32[]{:T(128)}, f32[2048,512]{1,0:T(8,128)}, f32[4,2048,64]{2,1,0:T(8,128)}, f32[4,64,64]{2,1,0:T(8,128)S(1)}, s32[]{:T(128)}, /*index=5*/s32[]{:T(128)}, s32[]{:T(128)}, s32[]{:T(128)}) while((s32[]{:T(128)}, f32[2048,512]{1,0:T(8,128)}, f32[4,2048,64]{2,1,0:T(8,128)}, f32[4,64,64]{2,1,0:T(8,128)S(1)}, s32[]{:T(128)}, ...), condition=%wide.region_3.3_spmd, body=%wide.region_1.2_spmd.sunk | while | flops 1636859904 | bytes 16023735 | solution.py:33
  259.1 117.9 %while.45 = (s32[]{:T(128)}, f32[2048,512]{1,0:T(8,128)}, f32[4,2048,64]{2,1,0:T(8,128)}, f32[4,64,64]{2,1,0:T(8,128)S(1)}, s32[]{:T(128)}, /*index=5*/s32[]{:T(128)}, s32[]{:T(128)}, s32[]{:T(128)}) while((s32[]{:T(128)}, f32[2048,512]{1,0:T(8,128)}, f32[4,2048,64]{2,1,0:T(8,128)}, f32[4,64,64]{2,1,0:T(8,128)S(1)}, s32[]{:T(128)}, ...), condition=%wide.region_3.3_spmd, body=%wide.region_1.2_spmd.sunk | while | flops 1636859904 | bytes 16023735 | solution.py:33
  389.4 22.1 all-gather.5.cloned.1.call-done
  411.5 117.9 %while.45 = (s32[]{:T(128)}, f32[2048,512]{1,0:T(8,128)}, f32[4,2048,64]{2,1,0:T(8,128)}, f32[4,64,64]{2,1,0:T(8,128)S(1)}, s32[]{:T(128)}, /*index=5*/s32[]{:T(128)}, s32[]{:T(128)}, s32[]{:T(128)}) while((s32[]{:T(128)}, f32[2048,512]{1,0:T(8,128)}, f32[4,2048,64]{2,1,0:T(8,128)}, f32[4,64,64]{2,1,0:T(8,128)S(1)}, s32[]{:T(128)}, ...), condition=%wide.region_3.3_spmd, body=%wide.region_1.2_spmd.sunk | while | flops 1636859904 | bytes 16023735 | solution.py:33
  541.8 22.1 all-gather.5.cloned.1.call-done
  563.9 117.8 %while.45 = (s32[]{:T(128)}, f32[2048,512]{1,0:T(8,128)}, f32[4,2048,64]{2,1,0:T(8,128)}, f32[4,64,64]{2,1,0:T(8,128)S(1)}, s32[]{:T(128)}, /*index=5*/s32[]{:T(128)}, s32[]{:T(128)}, s32[]{:T(128)}) while((s32[]{:T(128)}, f32[2048,512]{1,0:T(8,128)}, f32[4,2048,64]{2,1,0:T(8,128)}, f32[4,64,64]{2,1,0:T(8,128)S(1)}, s32[]{:T(128)}, ...), condition=%wide.region_3.3_spmd, body=%wide.region_1.2_spmd.sunk | while | flops 1636859904 | bytes 16023735 | solution.py:33
  716.3 117.9 %while.45 = (s32[]{:T(128)}, f32[2048,512]{1,0:T(8,128)}, f32[4,2048,64]{2,1,0:T(8,128)}, f32[4,64,64]{2,1,0:T(8,128)S(1)}, s32[]{:T(128)}, /*index=5*/s32[]{:T(128)}, s32[]{:T(128)}, s32[]{:T(128)}) while((s32[]{:T(128)}, f32[2048,512]{1,0:T(8,128)}, f32[4,2048,64]{2,1,0:T(8,128)}, f32[4,64,64]{2,1,0:T(8,128)S(1)}, s32[]{:T(128)}, ...), condition=%wide.region_3.3_spmd, body=%wide.region_1.2_spmd.sunk | while | flops 1636859904 | bytes 16023735 | solution.py:33
  868.7 117.9 %while.45 = (s32[]{:T(128)}, f32[2048,512]{1,0:T(8,128)}, f32[4,2048,64]{2,1,0:T(8,128)}, f32[4,64,64]{2,1,0:T(8,128)S(1)}, s32[]{:T(128)}, /*index=5*/s32[]{:T(128)}, s32[]{:T(128)}, s32[]{:T(128)}) while((s32[]{:T(128)}, f32[2048,512]{1,0:T(8,128)}, f32[4,2048,64]{2,1,0:T(8,128)}, f32[4,64,64]{2,1,0:T(8,128)S(1)}, s32[]{:T(128)}, ...), condition=%wide.region_3.3_spmd, body=%wide.region_1.2_spmd.sunk | while | flops 1636859904 | bytes 16023735 | solution.py:33
  999.0 22.1 all-gather.5.cloned.1.call-done
  1021.1 117.8 %while.45 = (s32[]{:T(128)}, f32[2048,512]{1,0:T(8,128)}, f32[4,2048,64]{2,1,0:T(8,128)}, f32[4,64,64]{2,1,0:T(8,128)S(1)}, s32[]{:T(128)}, /*index=5*/s32[]{:T(128)}, s32[]{:T(128)}, s32[]{:T(128)}) while((s32[]{:T(128)}, f32[2048,512]{1,0:T(8,128)}, f32[4,2048,64]{2,1,0:T(8,128)}, f32[4,64,64]{2,1,0:T(8,128)S(1)}, s32[]{:T(128)}, ...), condition=%wide.region_3.3_spmd, body=%wide.region_1.2_spmd.sunk | while | flops 1636859904 | bytes 16023735 | solution.py:33
  1173.5 117.9 %while.45 = (s32[]{:T(128)}, f32[2048,512]{1,0:T(8,128)}, f32[4,2048,64]{2,1,0:T(8,128)}, f32[4,64,64]{2,1,0:T(8,128)S(1)}, s32[]{:T(128)}, /*index=5*/s32[]{:T(128)}, s32[]{:T(128)}, s32[]{:T(128)}) while((s32[]{:T(128)}, f32[2048,512]{1,0:T(8,128)}, f32[4,2048,64]{2,1,0:T(8,128)}, f32[4,64,64]{2,1,0:T(8,128)S(1)}, s32[]{:T(128)}, ...), condition=%wide.region_3.3_spmd, body=%wide.region_1.2_spmd.sunk | while | flops 1636859904 | bytes 16023735 | solution.py:33
  1326.0 117.9 %while.45 = (s32[]{:T(128)}, f32[2048,512]{1,0:T(8,128)}, f32[4,2048,64]{2,1,0:T(8,128)}, f32[4,64,64]{2,1,0:T(8,128)S(1)}, s32[]{:T(128)}, /*index=5*/s32[]{:T(128)}, s32[]{:T(128)}, s32[]{:T(128)}) while((s32[]{:T(128)}, f32[2048,512]{1,0:T(8,128)}, f32[4,2048,64]{2,1,0:T(8,128)}, f32[4,64,64]{2,1,0:T(8,128)S(1)}, s32[]{:T(128)}, ...), condition=%wide.region_3.3_spmd, body=%wide.region_1.2_spmd.sunk | while | flops 1636859904 | bytes 16023735 | solution.py:33
  1456.2 22.1 all-gather.5.cloned.1.call-done
  1478.4 117.8 %while.45 = (s32[]{:T(128)}, f32[2048,512]{1,0:T(8,128)}, f32[4,2048,64]{2,1,0:T(8,128)}, f32[4,64,64]{2,1,0:T(8,128)S(1)}, s32[]{:T(128)}, /*index=5*/s32[]{:T(128)}, s32[]{:T(128)}, s32[]{:T(128)}) while((s32[]{:T(128)}, f32[2048,512]{1,0:T(8,128)}, f32[4,2048,64]{2,1,0:T(8,128)}, f32[4,64,64]{2,1,0:T(8,128)S(1)}, s32[]{:T(128)}, ...), condition=%wide.region_3.3_spmd, body=%wide.region_1.2_spmd.sunk | while | flops 1636859904 | bytes 16023735 | solution.py:33
  1630.8 117.9 %while.45 = (s32[]{:T(128)}, f32[2048,512]{1,0:T(8,128)}, f32[4,2048,64]{2,1,0:T(8,128)}, f32[4,64,64]{2,1,0:T(8,128)S(1)}, s32[]{:T(128)}, /*index=5*/s32[]{:T(128)}, s32[]{:T(128)}, s32[]{:T(128)}) while((s32[]{:T(128)}, f32[2048,512]{1,0:T(8,128)}, f32[4,2048,64]{2,1,0:T(8,128)}, f32[4,64,64]{2,1,0:T(8,128)S(1)}, s32[]{:T(128)}, ...), condition=%wide.region_3.3_spmd, body=%wide.region_1.2_spmd.sunk | while | flops 1636859904 | bytes 16023735 | solution.py:33
  1783.2 117.9 %while.45 = (s32[]{:T(128)}, f32[2048,512]{1,0:T(8,128)}, f32[4,2048,64]{2,1,0:T(8,128)}, f32[4,64,64]{2,1,0:T(8,128)S(1)}, s32[]{:T(128)}, /*index=5*/s32[]{:T(128)}, s32[]{:T(128)}, s32[]{:T(128)}) while((s32[]{:T(128)}, f32[2048,512]{1,0:T(8,128)}, f32[4,2048,64]{2,1,0:T(8,128)}, f32[4,64,64]{2,1,0:T(8,128)S(1)}, s32[]{:T(128)}, ...), condition=%wide.region_3.3_spmd, body=%wide.region_1.2_spmd.sunk | while | flops 1636859904 | bytes 16023735 | solution.py:33
  1913.5 22.1 all-gather.5.cloned.1.call-done
  1935.6 117.8 %while.45 = (s32[]{:T(128)}, f32[2048,512]{1,0:T(8,128)}, f32[4,2048,64]{2,1,0:T(8,128)}, f32[4,64,64]{2,1,0:T(8,128)S(1)}, s32[]{:T(128)}, /*index=5*/s32[]{:T(128)}, s32[]{:T(128)}, s32[]{:T(128)}) while((s32[]{:T(128)}, f32[2048,512]{1,0:T(8,128)}, f32[4,2048,64]{2,1,0:T(8,128)}, f32[4,64,64]{2,1,0:T(8,128)S(1)}, s32[]{:T(128)}, ...), condition=%wide.region_3.3_spmd, body=%wide.region_1.2_spmd.sunk | while | flops 1636859904 | bytes 16023735 | solution.py:33
  2088.0 117.9 %while.45 = (s32[]{:T(128)}, f32[2048,512]{1,0:T(8,128)}, f32[4,2048,64]{2,1,0:T(8,128)}, f32[4,64,64]{2,1,0:T(8,128)S(1)}, s32[]{:T(128)}, /*index=5*/s32[]{:T(128)}, s32[]{:T(128)}, s32[]{:T(128)}) while((s32[]{:T(128)}, f32[2048,512]{1,0:T(8,128)}, f32[4,2048,64]{2,1,0:T(8,128)}, f32[4,64,64]{2,1,0:T(8,128)S(1)}, s32[]{:T(128)}, ...), condition=%wide.region_3.3_spmd, body=%wide.region_1.2_spmd.sunk | while | flops 1636859904 | bytes 16023735 | solution.py:33
  2240.4 117.9 %while.45 = (s32[]{:T(128)}, f32[2048,512]{1,0:T(8,128)}, f32[4,2048,64]{2,1,0:T(8,128)}, f32[4,64,64]{2,1,0:T(8,128)S(1)}, s32[]{:T(128)}, /*index=5*/s32[]{:T(128)}, s32[]{:T(128)}, s32[]{:T(128)}) while((s32[]{:T(128)}, f32[2048,512]{1,0:T(8,128)}, f32[4,2048,64]{2,1,0:T(8,128)}, f32[4,64,64]{2,1,0:T(8,128)S(1)}, s32[]{:T(128)}, ...), condition=%wide.region_3.3_spmd, body=%wide.region_1.2_spmd.sunk | while | flops 1636859904 | bytes 16023735 | solution.py:33
  2370.7 22.1 all-gather.5.cloned.1.call-done
  2392.9 117.8 %while.45 = (s32[]{:T(128)}, f32[2048,512]{1,0:T(8,128)}, f32[4,2048,64]{2,1,0:T(8,128)}, f32[4,64,64]{2,1,0:T(8,128)S(1)}, s32[]{:T(128)}, /*index=5*/s32[]{:T(128)}, s32[]{:T(128)}, s32[]{:T(128)}) while((s32[]{:T(128)}, f32[2048,512]{1,0:T(8,128)}, f32[4,2048,64]{2,1,0:T(8,128)}, f32[4,64,64]{2,1,0:T(8,128)S(1)}, s32[]{:T(128)}, ...), condition=%wide.region_3.3_spmd, body=%wide.region_1.2_spmd.sunk | while | flops 1636859904 | bytes 16023735 | solution.py:33
  (477 shorter events, 2320.9 us)
Async XLA Ops:
  6.5 54.6 %all-to-all-start = ((f32[2,2048,256]{2,1,0:T(8,128)}), f32[2,2048,256]{2,1,0:T(8,128)}, u32[]{:S(2)}, u32[]{:S(2)}) async-start(f32[2,2048,256]{2,1,0:T(8,128)} %bitcast.32), calls=%async_computation | async-start | bytes 8388608 | tf_op jit(solution)/shard_map/all_to_all | solution.py:15
  71.9 34.9 %all-gather.5.cloned.1.call-start = ((), (), s32[]{:S(2)}) async-start(), calls=%async_computation.1 | async-start | bytes 5242880 | tf_op jit(solution)/shard_map/while/body/eval_jaxpr/all_gather | solution.py:21
  224.5 34.6 %all-gather.5.cloned.1.call-start = ((), (), s32[]{:S(2)}) async-start(), calls=%async_computation.1 | async-start | bytes 5242880 | tf_op jit(solution)/shard_map/while/body/eval_jaxpr/all_gather | solution.py:21
  318.0 21.5 all-reduce.2.cloned.1.call-start
  376.9 34.6 %all-gather.5.cloned.1.call-start = ((), (), s32[]{:S(2)}) async-start(), calls=%async_computation.1 | async-start | bytes 5242880 | tf_op jit(solution)/shard_map/while/body/eval_jaxpr/all_gather | solution.py:21
  499.8 21.5 all-reduce.2.cloned.1.call-start
  529.3 34.6 %all-gather.5.cloned.1.call-start = ((), (), s32[]{:S(2)}) async-start(), calls=%async_computation.1 | async-start | bytes 5242880 | tf_op jit(solution)/shard_map/while/body/eval_jaxpr/all_gather | solution.py:21
  681.7 34.6 %all-gather.5.cloned.1.call-start = ((), (), s32[]{:S(2)}) async-start(), calls=%async_computation.1 | async-start | bytes 5242880 | tf_op jit(solution)/shard_map/while/body/eval_jaxpr/all_gather | solution.py:21
  775.2 21.5 all-reduce.2.cloned.1.call-start
  834.2 34.6 %all-gather.5.cloned.1.call-start = ((), (), s32[]{:S(2)}) async-start(), calls=%async_computation.1 | async-start | bytes 5242880 | tf_op jit(solution)/shard_map/while/body/eval_jaxpr/all_gather | solution.py:21
  957.1 21.5 all-reduce.2.cloned.1.call-start
  986.6 34.6 %all-gather.5.cloned.1.call-start = ((), (), s32[]{:S(2)}) async-start(), calls=%async_computation.1 | async-start | bytes 5242880 | tf_op jit(solution)/shard_map/while/body/eval_jaxpr/all_gather | solution.py:21
  1139.0 34.6 %all-gather.5.cloned.1.call-start = ((), (), s32[]{:S(2)}) async-start(), calls=%async_computation.1 | async-start | bytes 5242880 | tf_op jit(solution)/shard_map/while/body/eval_jaxpr/all_gather | solution.py:21
  1232.4 21.5 all-reduce.2.cloned.1.call-start
  1291.4 34.6 %all-gather.5.cloned.1.call-start = ((), (), s32[]{:S(2)}) async-start(), calls=%async_computation.1 | async-start | bytes 5242880 | tf_op jit(solution)/shard_map/while/body/eval_jaxpr/all_gather | solution.py:21
  1414.3 21.5 all-reduce.2.cloned.1.call-start
  1443.8 34.6 %all-gather.5.cloned.1.call-start = ((), (), s32[]{:S(2)}) async-start(), calls=%async_computation.1 | async-start | bytes 5242880 | tf_op jit(solution)/shard_map/while/body/eval_jaxpr/all_gather | solution.py:21
  1596.2 34.6 %all-gather.5.cloned.1.call-start = ((), (), s32[]{:S(2)}) async-start(), calls=%async_computation.1 | async-start | bytes 5242880 | tf_op jit(solution)/shard_map/while/body/eval_jaxpr/all_gather | solution.py:21
  1748.6 34.6 %all-gather.5.cloned.1.call-start = ((), (), s32[]{:S(2)}) async-start(), calls=%async_computation.1 | async-start | bytes 5242880 | tf_op jit(solution)/shard_map/while/body/eval_jaxpr/all_gather | solution.py:21
  1901.1 34.6 %all-gather.5.cloned.1.call-start = ((), (), s32[]{:S(2)}) async-start(), calls=%async_computation.1 | async-start | bytes 5242880 | tf_op jit(solution)/shard_map/while/body/eval_jaxpr/all_gather | solution.py:21
  2053.4 34.6 %all-gather.5.cloned.1.call-start = ((), (), s32[]{:S(2)}) async-start(), calls=%async_computation.1 | async-start | bytes 5242880 | tf_op jit(solution)/shard_map/while/body/eval_jaxpr/all_gather | solution.py:21
  2205.9 34.6 %all-gather.5.cloned.1.call-start = ((), (), s32[]{:S(2)}) async-start(), calls=%async_computation.1 | async-start | bytes 5242880 | tf_op jit(solution)/shard_map/while/body/eval_jaxpr/all_gather | solution.py:21
  2328.8 21.5 all-reduce.2.cloned.1.call-start
  2358.3 34.6 %all-gather.5.cloned.1.call-start = ((), (), s32[]{:S(2)}) async-start(), calls=%async_computation.1 | async-start | bytes 5242880 | tf_op jit(solution)/shard_map/while/body/eval_jaxpr/all_gather | solution.py:21
  (57 other events, 1224.6 us)
Sparse Core Ops, SparseCore 0:
  74.5 32.1 all-gather.4
  227.2 31.8 all-gather.4
  323.6 15.7 all-reduce.1
  379.6 31.8 all-gather.4
  505.5 15.7 all-reduce.1
  532.0 31.8 all-gather.4
  684.4 31.8 all-gather.4
  780.9 15.7 all-reduce.1
  836.8 31.8 all-gather.4
  962.7 15.7 all-reduce.1
  989.3 31.8 all-gather.4
  1141.7 31.8 all-gather.4
  1238.1 15.7 all-reduce.1
  1294.1 31.8 all-gather.4
  1420.0 15.7 all-reduce.1
  1446.5 31.8 all-gather.4
  1598.9 31.8 all-gather.4
  1695.3 15.7 all-reduce.1
  1751.3 31.8 all-gather.4
  1877.2 15.7 all-reduce.1
  1903.7 31.8 all-gather.4
  2056.1 31.8 all-gather.4
  2208.6 31.8 all-gather.4
  2361.0 31.8 all-gather.4
  (56 shorter events, 880.4 us)
where the time goes:
time: 2520 us
  waiting for transfers between devices  1420 us (56%)
  matrix products  863 us (34%)
  blocking collectives  146 us (6%)
  local copies, waits for them, and re-layouts  63.5 us (3%)
    psum x64, waiting for transfers between devices, panel_step(): w_full = lax.psum(w_part, 'row')  1020 us
    dot_general x64, matrix products, panel_step(): jnp.dot(v_j, y_mat, precision=HIGHEST, preferred_element_type=jnp.float32)  435 us
    all_gather x16, waiting for transfers between devices, group_step(): v_group = lax.all_gather(v_blk, 'col', axis=0)  354 us
    dot_general x64, matrix products, panel_step(): jnp.einsum('na,nk->ak', v_j, x_in, precision=HIGHEST, preferred_element_t...  353 us
    all_gather x16, blocking collectives, group_step(): t_group = lax.all_gather(t_blk, 'col', axis=0)  146 us
    dot_general x64, matrix products, panel_step(): jnp.dot(t_j, w_full, precision=HIGHEST, preferred_element_type=jnp.float32)  74.6 us
  transfers between devices with their start and end apart: 81, of which 81 were waited for; matrix products, arithmetic and copies ran while one was open for 0% of the time, Pallas kernels for 0%

commit v1 on v0

v1 whole, which is shorter than its diff:
```python
import jax
import jax.numpy as jnp
from jax import lax
from jax.experimental import pallas as pl
from jax.experimental.pallas import tpu as pltpu
from jax.sharding import PartitionSpec as P

F32 = jnp.float32
BF16 = jnp.bfloat16
MESH = pl.DeviceIdType.MESH
PW = 64
RB = 256
GROUPS = 8
BLOCKS = GROUPS * (GROUPS + 1) // 2
HALF = RB // 2
AHEAD_W = 3
OWN_LEAD = 2
COLS = 256
ROWS = 2048
GW = GROUPS * PW
HW = GW // 2
VMEM_LIMIT = 66 * 10**6


def split3(x):
    a = x.astype(BF16)
    r = x - a.astype(F32)
    b = r.astype(BF16)
    c = (r - b.astype(F32)).astype(BF16)
    return a, b, c


def dot6(lhs, rhs):
    a1, a2, a3 = lhs
    b1, b2, b3 = rhs

    def mm(p, q):
        return jnp.dot(p, q, preferred_element_type=F32)

    return ((mm(a3, b1) + mm(a1, b3)) + mm(a2, b2)) + (mm(a2, b1) + mm(a1, b2)) + mm(a1, b1)


def dot_f32(a, b):
    return dot6(split3(a), split3(b))


def kernel(v_hbm, t_hbm, z_hbm, out_hbm, v_buf, t_buf, x_buf, w0, w1, g00, g01, g11, y_buf,
           loc_sem, t_send, t_recv, send, recv, c_send, c_recv, io_sem):
    row = lax.axis_index('row')
    col = lax.axis_index('col')
    orow = 1 - row
    xcol = lax.rem(col + 2, 4)
    pcol = col + 1 - 2 * lax.rem(col, 2)
    x_dev, y_dev, p_dev = (row, xcol), (orow, col), (row, pcol)
    me = row * 4 + col
    xs = row * 4 + xcol
    ys = orow * 4 + col
    ds = orow * 4 + xcol

    def vmem(slot, blk, off=0, size=RB):
        return v_buf.at[slot, pl.ds(pl.multiple_of(blk * RB + off, HALF), size), :]

    def rcopy(slot, blk, kind, dev, off=0, size=RB):
        return pltpu.make_async_remote_copy(
            src_ref=vmem(slot, blk, off, size), dst_ref=vmem(slot, blk, off, size),
            send_sem=send.at[kind, blk], recv_sem=recv.at[kind, blk], device_id=dev, device_id_type=MESH)

    OX, OY, OP, FX, FY, PX, PY, PD = range(8)

    def own(blk):
        return (rcopy(me, blk, OX, x_dev), rcopy(me, blk, OY, y_dev), rcopy(me, blk, OP, p_dev))

    def fwd(blk):
        return (rcopy(xs, blk, FY, y_dev, 0, HALF), rcopy(ys, blk, FX, x_dev, HALF, HALF),
                rcopy(xs, blk, PX, p_dev), rcopy(ys, blk, PY, p_dev))

    def diag(blk):
        return rcopy(ds, blk, PD, p_dev)

    def t_copy(slot, kind, dev):
        return pltpu.make_async_remote_copy(
            src_ref=t_buf.at[slot], dst_ref=t_buf.at[slot], send_sem=t_send.at[kind], recv_sem=t_recv.at[kind],
            device_id=dev, device_id_type=MESH)

    def local_v(n):
        k = GROUPS - n
        o = n * (n - 1) // 2
        return pltpu.make_async_copy(
            v_hbm.at[pl.ds(RB * k, RB * n), pl.ds(2 * PW * k, 2 * PW)],
            v_buf.at[me, pl.ds(RB * o, RB * n), :], loc_sem.at[n - 1])

    for n in range(1, GROUPS + 1):
        local_v(n).start()
    t_in = pltpu.make_async_copy(t_hbm, t_buf.at[col], io_sem.at[0])
    t_in.start()
    z_in = pltpu.make_async_copy(z_hbm, x_buf, io_sem.at[1])
    z_in.start()

    barrier = pltpu.get_barrier_semaphore()
    for dev in (x_dev, y_dev, p_dev):
        pl.semaphore_signal(barrier, inc=1, device_id=dev, device_id_type=MESH)
    pl.semaphore_wait(barrier, 3)

    for n in range(1, GROUPS + 1):
        local_v(n).wait()
        if n == 2:
            for b in range(OWN_LEAD):
                for c in own(b):
                    c.start()
            t_in.wait()
            t_copy(col, 0, x_dev).start()
            t_copy(col, 1, p_dev).start()
    z_in.wait()

    def pump(blk, _):
        rcopy(xs, blk, OX, x_dev).wait_recv()
        rcopy(ys, blk, OY, y_dev).wait_recv()
        for c in fwd(blk):
            c.start()

        @pl.when(blk + OWN_LEAD < BLOCKS)
        def _():
            for c in own(blk + OWN_LEAD):
                c.start()
        return 0

    def pump_to(done, target):
        target = jnp.maximum(done, jnp.minimum(target, BLOCKS))
        lax.fori_loop(done, target, pump, 0)
        return target

    def take_diag(blk):
        rcopy(ds, blk, FY, y_dev, 0, HALF).wait_recv()
        rcopy(ds, blk, FX, x_dev, HALF, HALF).wait_recv()
        diag(blk).start()

    def need(blk):
        rcopy(me, blk, OP, p_dev).wait_recv()
        rcopy(me, blk, PX, p_dev).wait_recv()
        rcopy(me, blk, PY, p_dev).wait_recv()
        rcopy(me, blk, PD, p_dev).wait_recv()

    lane = lax.broadcasted_iota(jnp.int32, (RB, 128), 1)

    def halves(dd, blk):
        r = pl.ds(pl.multiple_of(blk * RB, RB), RB)
        tiles = [v_buf[dd * 4 + e, r, :] for e in range(4)]
        rolled = [pltpu.roll(t, PW, 1) for t in tiles]
        low = [jnp.where(lane < PW, tiles[e], rolled[e + 1]) for e in (0, 2)]
        high = [jnp.where(lane < PW, rolled[e], tiles[e + 1]) for e in (0, 2)]
        return jnp.concatenate(low, axis=1), jnp.concatenate(high, axis=1)

    ri = lax.broadcasted_iota(jnp.int32, (HW, HW), 0) // PW
    ci = lax.broadcasted_iota(jnp.int32, (HW, HW), 1) // PW
    near = jnp.logical_and(ri // 2 == ci // 2, ri < ci)
    far = ri // 2 < ci // 2

    def block_t(k, par):
        rows = []
        for e in range(4):
            t = t_buf[e, pl.ds(pl.multiple_of(k * PW, PW), PW), :]
            r = pltpu.roll(t, PW, 1)
            src = t if par == e % 2 else r
            keep = lax.broadcasted_iota(jnp.int32, (PW, 128), 1) // PW == e % 2
            tile = jnp.where(keep, src, 0.0)
            zero = jnp.zeros((PW, 128), F32)
            rows.append(jnp.concatenate([tile, zero] if e < 2 else [zero, tile], axis=1))
        return jnp.concatenate(rows, axis=0)

    def merge(t, g):
        t = t - dot_f32(t, dot_f32(jnp.where(near, g, 0.0), t))
        return t - dot_f32(t, dot_f32(jnp.where(far, g, 0.0), t))

    def group(step, carry):
        pumped, diag_done = carry
        n = step + 1
        k = GROUPS - n
        first = n * step // 2
        w0[...] = jnp.zeros_like(w0)
        w1[...] = jnp.zeros_like(w1)
        g00[...] = jnp.zeros_like(g00)
        g01[...] = jnp.zeros_like(g01)
        g11[...] = jnp.zeros_like(g11)

        def gather_step(i, carry):
            pumped, diag_done = carry
            blk = first + i
            pumped = pump_to(pumped, blk + AHEAD_W)

            def dg(b, _):
                take_diag(b)
                return 0
            diag_to = jnp.minimum(blk + 2, BLOCKS)
            lax.fori_loop(diag_done, diag_to, dg, 0)
            need(blk)
            r = pl.ds(pl.multiple_of((k + i) * RB, RB), RB)
            parts = [halves(dd, blk) for dd in range(2)]
            v0 = split3(jnp.concatenate([p[0] for p in parts], axis=0))
            v1 = split3(jnp.concatenate([p[1] for p in parts], axis=0))
            x = split3(jnp.concatenate([x_buf[0, r, :], x_buf[1, r, :]], axis=0))
            t0 = [t.T for t in v0]
            t1 = [t.T for t in v1]
            w0[...] += dot6(t0, x)
            w1[...] += dot6(t1, x)
            g00[...] += dot6(t0, v0)
            g01[...] += dot6(t0, v1)
            g11[...] += dot6(t1, v1)
            return pumped, diag_to

        pumped, diag_done = lax.fori_loop(0, n, gather_step, (pumped, diag_done))

        @pl.when(step == 0)
        def _():
            t_copy(xcol, 0, x_dev).wait_recv()
            t_copy(xcol, 2, p_dev).start()
            t_copy(pcol, 1, p_dev).wait_recv()
            t_copy(lax.rem(pcol + 2, 4), 2, p_dev).wait_recv()

        ta = merge(block_t(k, 0), g00[...])
        tb = merge(block_t(k, 1), g11[...])
        y1 = dot_f32(tb, w1[...])
        y0 = dot_f32(ta, w0[...] - dot_f32(g01[...], y1))
        for e in range(4):
            y_buf[e * 128:e * 128 + PW, :] = y0[e * PW:(e + 1) * PW]
            y_buf[e * 128 + PW:(e + 1) * 128, :] = y1[e * PW:(e + 1) * PW]

        def update_step(i, pumped):
            blk = first + i
            pumped = pump_to(pumped, first + n - 1 + AHEAD_W + (i + 1) // 2)
            rv = pl.ds(pl.multiple_of(blk * RB, RB), RB)
            rx = pl.ds(pl.multiple_of((k + i) * RB, RB), RB)
            v = jnp.concatenate(
                [jnp.concatenate([v_buf[dd * 4 + e, rv, :] for e in range(4)], axis=1) for dd in range(2)], axis=0)
            delta = dot6(split3(v), split3(y_buf[...]))
            x_buf[0, rx, :] = x_buf[0, rx, :] - delta[:RB]
            x_buf[1, rx, :] = x_buf[1, rx, :] - delta[RB:]

            @pl.when(jnp.logical_and(k == 0, i > 0))
            def _():
                give(i - 1).start()
            return pumped

        pumped = lax.fori_loop(0, n, update_step, pumped)
        return pumped, diag_done

    def give(i):
        r = pl.ds(pl.multiple_of(i * RB, RB), RB)
        return pltpu.make_async_remote_copy(
            src_ref=x_buf.at[orow, r, :],
            dst_ref=out_hbm.at[r, pl.ds(pl.multiple_of(row * COLS, COLS), COLS)],
            send_sem=c_send.at[i], recv_sem=c_recv.at[i], device_id=y_dev, device_id_type=MESH)

    lax.fori_loop(0, GROUPS, group, (0, 0))

    def drain(blk, _):
        for c in own(blk):
            c.wait_send()
        for c in fwd(blk):
            c.wait_send()
        diag(blk).wait_send()
        return 0
    lax.fori_loop(0, BLOCKS, drain, 0)
    t_copy(col, 0, x_dev).wait_send()
    t_copy(col, 1, p_dev).wait_send()
    t_copy(xcol, 2, p_dev).wait_send()

    give(GROUPS - 1).start()
    keep = pltpu.make_async_copy(
        x_buf.at[row], out_hbm.at[:, pl.ds(pl.multiple_of(row * COLS, COLS), COLS)], io_sem.at[2])
    keep.start()
    keep.wait()

    def drain_c(i, _):
        give(i).wait()
        return 0
    lax.fori_loop(0, GROUPS, drain_c, 0)


def solution(mesh):
    def local_apply(v_loc, t_loc, z_loc):
        t_pk = t_loc.reshape(GROUPS, 2, PW, PW).transpose(0, 2, 1, 3).reshape(GROUPS * PW, 2 * PW)
        z_pk = z_loc.reshape(2, ROWS, COLS)
        any_spec = pl.BlockSpec(memory_space=pl.ANY)
        return pl.pallas_call(
            kernel,
            out_shape=jax.ShapeDtypeStruct((ROWS, 2 * COLS), F32),
            in_specs=[any_spec] * 3,
            out_specs=any_spec,
            scratch_shapes=[
                pltpu.VMEM((8, BLOCKS * RB, 128), F32),
                pltpu.VMEM((4, GROUPS * PW, 128), F32),
                pltpu.VMEM((2, ROWS, COLS), F32),
                pltpu.VMEM((HW, COLS), F32),
                pltpu.VMEM((HW, COLS), F32),
                pltpu.VMEM((HW, HW), F32),
                pltpu.VMEM((HW, HW), F32),
                pltpu.VMEM((HW, HW), F32),
                pltpu.VMEM((GW, COLS), F32),
                pltpu.SemaphoreType.DMA((GROUPS,)),
                pltpu.SemaphoreType.DMA((3,)),
                pltpu.SemaphoreType.DMA((3,)),
                pltpu.SemaphoreType.DMA((8, BLOCKS)),
                pltpu.SemaphoreType.DMA((8, BLOCKS)),
                pltpu.SemaphoreType.DMA((GROUPS,)),
                pltpu.SemaphoreType.DMA((GROUPS,)),
                pltpu.SemaphoreType.DMA((3,)),
            ],
            compiler_params=pltpu.CompilerParams(
                collective_id=0, has_side_effects=True, vmem_limit_bytes=VMEM_LIMIT),
            name='panels',
        )(v_loc, t_pk, z_pk)

    return jax.shard_map(local_apply, mesh=mesh,
                         in_specs=(P('row', 'col'), P('col', None, None), P(None, ('col', 'row'))),
                         out_specs=P('row', 'col'), check_vma=False)
```

time: 2520 us -> 272 us (0.11)
  waiting for transfers between devices: 1420 us -> 0 us
  matrix products: 863 us -> 0 us
  Pallas kernels: 0 us -> 264 us
  blocking collectives: 146 us -> 0 us
  local copies, waits for them, and re-layouts: 63.5 us -> 7.11 us
    psum x64 -> x0, waiting for transfers between devices: 1020 us -> none  [panel_step(): w_full = lax.psum(w_part, 'row')]
    dot_general x192 -> x0, matrix products: 863 us -> none  [the longest x64 435 us: panel_step(): jnp.dot(v_j, y_mat, precision=HIGHEST, preferred_element_type=jnp.float32)]
    all_gather x16 -> x0, waiting for transfers between devices: 354 us -> none  [group_step(): v_group = lax.all_gather(v_blk, 'col', axis=0)]
    pallas_call x0 -> x1, Pallas kernels: none -> 264 us  [local_apply(): pl.pallas_call(kernel, out_shape=jax.ShapeDtypeStruct((ROWS, 2 * COLS), F...]
    all_gather x16 -> x0, blocking collectives: 146 us -> none  [group_step(): t_group = lax.all_gather(t_blk, 'col', axis=0)]
    dynamic_slice x32 -> x0, local copies, waits for them, and re-layouts: 52.7 us -> none  [the longest x16 40.5 us: group_step(): lax.dynamic_slice_in_dim(v_loc, group_idx * panel_width, panel_width, axi...]
    all_to_all x1 -> x0, waiting for transfers between devices: 48.9 us -> none  [local_apply(): x_loc = lax.all_to_all(z_loc, 'row', 0, 1, tiled=True)]
  transfers between devices with their start and end apart: 81 -> 0, of which waited for: 81 -> 0; matrix products, arithmetic and copies ran while one was open for 0% -> 0% of each run, Pallas kernels for 0% -> 0%
where the time goes in v1:
time: 272 us
  Pallas kernels  264 us (97%)
  local copies, waits for them, and re-layouts  7.11 us (3%)
    pallas_call x1, Pallas kernels, local_apply(): pl.pallas_call(kernel, out_shape=jax.ShapeDtypeStruct((ROWS, 2 * COLS), F...  264 us

profile of v1, /device:TPU:0, one launch (start us, length us, event | category | flops | bytes accessed | tf_op | source)
XLA Modules:
  0.0 271.6 jit_solution(3064622314808202473)
XLA Ops:
  0.0 1.4 copy.6
  1.5 1.0 reshape.10.t_hbm
  2.5 264.5 %panels.1 = f32[2048,512]{1,0:T(8,128)} custom-call(f32[2048,1024]{1,0:T(8,128)} %v_hbm.1, f32[512,128]{1,0:T(8,128)} %reshape.10.t_hbm, f32[2,2048,256]{2,1,0:T(8,128)} %bitcast.5), custom_call_target="tpu_custom_call" | custom-call | tf_op jit(solution)/shard_map/panels/pallas_call | solution.py:284
  266.9 4.6 %copy.8 = f32[2048,512]{1,0:T(8,128)} copy(f32[2048,512]{1,0:T(8,128)} %panels.1) | data formatting | bytes 8388608

commit v2 on v1

--- a/solution.py
+++ b/solution.py
@@ -13,8 +13,8 @@
 GROUPS = 8
 BLOCKS = GROUPS * (GROUPS + 1) // 2
 HALF = RB // 2
-AHEAD_W = 3
-OWN_LEAD = 2
+AHEAD_W = 5
+OWN_LEAD = 4
 COLS = 256
 ROWS = 2048
 GW = GROUPS * PW
@@ -44,13 +44,14 @@
     return dot6(split3(a), split3(b))
 
 
-def kernel(v_hbm, t_hbm, z_hbm, out_hbm, v_buf, t_buf, x_buf, w0, w1, g00, g01, g11, y_buf,
-           loc_sem, t_send, t_recv, send, recv, c_send, c_recv, io_sem):
+def kernel(v_hbm, t_hbm, z_hbm, out_hbm, v_buf, t_buf, x_buf, w_buf, g_part, g_in, g_last, y_buf,
+           loc_sem, t_send, t_recv, send, recv, g_send, g_recv, c_send, c_recv, io_sem):
     row = lax.axis_index('row')
     col = lax.axis_index('col')
     orow = 1 - row
     xcol = lax.rem(col + 2, 4)
-    pcol = col + 1 - 2 * lax.rem(col, 2)
+    core = lax.rem(col, 2)
+    pcol = col + 1 - 2 * core
     x_dev, y_dev, p_dev = (row, xcol), (orow, col), (row, pcol)
     me = row * 4 + col
     xs = row * 4 + xcol
@@ -103,7 +104,7 @@
 
     for n in range(1, GROUPS + 1):
         local_v(n).wait()
-        if n == 2:
+        if n == 4:
             for b in range(OWN_LEAD):
                 for c in own(b):
                     c.start()
@@ -140,49 +141,76 @@
         rcopy(me, blk, PY, p_dev).wait_recv()
         rcopy(me, blk, PD, p_dev).wait_recv()
 
-    lane = lax.broadcasted_iota(jnp.int32, (RB, 128), 1)
-
-    def halves(dd, blk):
+    def rows_of(blk, dds):
         r = pl.ds(pl.multiple_of(blk * RB, RB), RB)
-        tiles = [v_buf[dd * 4 + e, r, :] for e in range(4)]
-        rolled = [pltpu.roll(t, PW, 1) for t in tiles]
-        low = [jnp.where(lane < PW, tiles[e], rolled[e + 1]) for e in (0, 2)]
-        high = [jnp.where(lane < PW, rolled[e], tiles[e + 1]) for e in (0, 2)]
-        return jnp.concatenate(low, axis=1), jnp.concatenate(high, axis=1)
-
-    ri = lax.broadcasted_iota(jnp.int32, (HW, HW), 0) // PW
-    ci = lax.broadcasted_iota(jnp.int32, (HW, HW), 1) // PW
-    near = jnp.logical_and(ri // 2 == ci // 2, ri < ci)
-    far = ri // 2 < ci // 2
-
-    def block_t(k, par):
-        rows = []
+        return jnp.concatenate(
+            [jnp.concatenate([v_buf[dd * 4 + e, r, :] for e in range(4)], axis=1) for dd in dds], axis=0)
+
+    def gram(cols, vals):
+        first = [t[:HW] for t in cols]
+        last = [t[HW:] for t in cols]
+        vf = [v[:, :HW] for v in vals]
+        vl = [v[:, HW:] for v in vals]
+        return dot6(first, vf), dot6(first, vl), dot6(last, vl)
+
+    lane = lax.broadcasted_iota(jnp.int32, (HW, 128), 1)
+    lane_t = lax.broadcasted_iota(jnp.int32, (PW, 128), 1)
+    zero_t = jnp.zeros((PW, 128), F32)
+
+    def lanes_of(q, par):
+        a, b = q[:, :128], q[:, 128:]
+        if par == 0:
+            return jnp.where(lane < PW, a, pltpu.roll(b, PW, 1))
+        return jnp.where(lane < PW, pltpu.roll(a, PW, 1), b)
+
+    def rows_par(q, par):
+        return jnp.concatenate([q[par * PW:(par + 1) * PW], q[128 + par * PW:128 + (par + 1) * PW]], axis=0)
+
+    def factors(k, par):
+        tiles = []
         for e in range(4):
             t = t_buf[e, pl.ds(pl.multiple_of(k * PW, PW), PW), :]
-            r = pltpu.roll(t, PW, 1)
-            src = t if par == e % 2 else r
-            keep = lax.broadcasted_iota(jnp.int32, (PW, 128), 1) // PW == e % 2
-            tile = jnp.where(keep, src, 0.0)
-            zero = jnp.zeros((PW, 128), F32)
-            rows.append(jnp.concatenate([tile, zero] if e < 2 else [zero, tile], axis=1))
-        return jnp.concatenate(rows, axis=0)
-
-    def merge(t, g):
-        t = t - dot_f32(t, dot_f32(jnp.where(near, g, 0.0), t))
-        return t - dot_f32(t, dot_f32(jnp.where(far, g, 0.0), t))
+            src = t if par == e % 2 else pltpu.roll(t, PW, 1)
+            tiles.append(jnp.where(lane_t // PW == e % 2, src, 0.0))
+        return tiles
+
+    def diag256(tiles):
+        return jnp.concatenate(
+            [jnp.concatenate([t, zero_t] if e < 2 else [zero_t, t], axis=1) for e, t in enumerate(tiles)], axis=0)
+
+    def merge(tiles, gaa, gab, gbb):
+        whole = diag256(tiles)
+        u = jnp.concatenate([jnp.where(lane_t < PW, 0.0, gaa[:PW]), jnp.where(lane_t < PW, 0.0, gbb[:PW])], axis=1)
+        c = dot_f32(u, whole)
+        rhs = jnp.concatenate([
+            jnp.concatenate([c[:, :128], zero_t], axis=1), jnp.zeros((PW, HW), F32),
+            jnp.concatenate([zero_t, c[:, 128:]], axis=1), jnp.zeros((PW, HW), F32)], axis=0)
+        lhs = jnp.concatenate([tiles[0] + tiles[1], tiles[2] + tiles[3]], axis=1)
+        p = dot_f32(lhs, rhs)
+        ta = jnp.concatenate([tiles[0] - p[:, :128], tiles[1]], axis=0)
+        tb = jnp.concatenate([tiles[2] - p[:, 128:], tiles[3]], axis=0)
+        tab = dot_f32(ta, dot_f32(gab, tb))
+        return jnp.concatenate([
+            jnp.concatenate([ta, -tab], axis=1), jnp.concatenate([jnp.zeros_like(tb), tb], axis=1)], axis=0)
+
+    def g_copy(n):
+        return pltpu.make_async_remote_copy(
+            src_ref=g_part, dst_ref=g_in.at[lax.rem(n, 2)], send_sem=g_send, recv_sem=g_recv.at[lax.rem(n, 2)],
+            device_id=p_dev, device_id_type=MESH)
 
     def group(step, carry):
         pumped, diag_done = carry
         n = step + 1
         k = GROUPS - n
         first = n * step // 2
-        w0[...] = jnp.zeros_like(w0)
-        w1[...] = jnp.zeros_like(w1)
-        g00[...] = jnp.zeros_like(g00)
-        g01[...] = jnp.zeros_like(g01)
-        g11[...] = jnp.zeros_like(g11)
-
-        def gather_step(i, carry):
+        w_buf[...] = jnp.zeros_like(w_buf)
+
+        @pl.when(n > 2)
+        def _():
+            g_copy(n - 1).wait_send()
+        g_part[...] = jnp.zeros_like(g_part)
+
+        def arrive(i, carry):
             pumped, diag_done = carry
             blk = first + i
             pumped = pump_to(pumped, blk + AHEAD_W)
@@ -193,21 +221,34 @@
             diag_to = jnp.minimum(blk + 2, BLOCKS)
             lax.fori_loop(diag_done, diag_to, dg, 0)
             need(blk)
+            return pumped, diag_to
+
+        def load(i):
             r = pl.ds(pl.multiple_of((k + i) * RB, RB), RB)
-            parts = [halves(dd, blk) for dd in range(2)]
-            v0 = split3(jnp.concatenate([p[0] for p in parts], axis=0))
-            v1 = split3(jnp.concatenate([p[1] for p in parts], axis=0))
-            x = split3(jnp.concatenate([x_buf[0, r, :], x_buf[1, r, :]], axis=0))
-            t0 = [t.T for t in v0]
-            t1 = [t.T for t in v1]
-            w0[...] += dot6(t0, x)
-            w1[...] += dot6(t1, x)
-            g00[...] += dot6(t0, v0)
-            g01[...] += dot6(t0, v1)
-            g11[...] += dot6(t1, v1)
-            return pumped, diag_to
-
-        pumped, diag_done = lax.fori_loop(0, n, gather_step, (pumped, diag_done))
+            v = split3(rows_of(first + i, (core, 1 - core)))
+            x = split3(jnp.concatenate([x_buf[core, r, :], x_buf[1 - core, r, :]], axis=0))
+            t = [p.T for p in v]
+            w_buf[...] += dot6(t, x)
+            return v, t
+
+        def gather_step(i, carry):
+            carry = arrive(i, carry)
+            v, t = load(i)
+            gs = gram([p[:, :RB] for p in t], [p[:RB] for p in v])
+            for q in range(3):
+                g_part[q] += gs[q]
+            return carry
+
+        carry = lax.fori_loop(0, step, gather_step, (pumped, diag_done))
+        pumped, diag_done = arrive(step, carry)
+
+        @pl.when(step > 0)
+        def _():
+            g_copy(n).start()
+        v, t = load(step)
+        gs = gram(t, v)
+        for q in range(3):
+            g_last[q] = gs[q]
 
         @pl.when(step == 0)
         def _():
@@ -216,22 +257,30 @@
             t_copy(pcol, 1, p_dev).wait_recv()
             t_copy(lax.rem(pcol + 2, 4), 2, p_dev).wait_recv()
 
-        ta = merge(block_t(k, 0), g00[...])
-        tb = merge(block_t(k, 1), g11[...])
-        y1 = dot_f32(tb, w1[...])
-        y0 = dot_f32(ta, w0[...] - dot_f32(g01[...], y1))
+        @pl.when(step > 0)
+        def _():
+            g_copy(n).wait_recv()
+            for q in range(3):
+                g_last[q] += g_part[q] + g_in[lax.rem(n, 2), q]
+        lanes = [[lanes_of(g_last[q], par) for par in range(2)] for q in range(3)]
+        ts = [merge(factors(k, par), *[rows_par(lanes[q][par], par) for q in range(3)]) for par in range(2)]
+        g01 = jnp.concatenate([
+            jnp.concatenate([rows_par(lanes[0][1], 0), rows_par(lanes[1][1], 0)], axis=1),
+            jnp.concatenate([rows_par(lanes[1][0], 1).T, rows_par(lanes[2][1], 0)], axis=1)], axis=0)
+        w0, w1 = [jnp.concatenate([w_buf[e * 128 + par * PW:e * 128 + (par + 1) * PW, :] for e in range(4)], axis=0)
+                  for par in range(2)]
+        y1 = dot_f32(ts[1], w1)
+        y0 = dot_f32(ts[0], w0 - dot_f32(g01, y1))
         for e in range(4):
-            y_buf[e * 128:e * 128 + PW, :] = y0[e * PW:(e + 1) * PW]
-            y_buf[e * 128 + PW:(e + 1) * 128, :] = y1[e * PW:(e + 1) * PW]
+            for par, y in enumerate((y0, y1)):
+                for q, part in enumerate(split3(y[e * PW:(e + 1) * PW])):
+                    y_buf[q, e * 128 + par * PW:e * 128 + (par + 1) * PW, :] = part
 
         def update_step(i, pumped):
             blk = first + i
             pumped = pump_to(pumped, first + n - 1 + AHEAD_W + (i + 1) // 2)
-            rv = pl.ds(pl.multiple_of(blk * RB, RB), RB)
             rx = pl.ds(pl.multiple_of((k + i) * RB, RB), RB)
-            v = jnp.concatenate(
-                [jnp.concatenate([v_buf[dd * 4 + e, rv, :] for e in range(4)], axis=1) for dd in range(2)], axis=0)
-            delta = dot6(split3(v), split3(y_buf[...]))
+            delta = dot6(split3(rows_of(blk, (0, 1))), [y_buf[q] for q in range(3)])
             x_buf[0, rx, :] = x_buf[0, rx, :] - delta[:RB]
             x_buf[1, rx, :] = x_buf[1, rx, :] - delta[RB:]
 
@@ -263,6 +312,7 @@
     t_copy(col, 0, x_dev).wait_send()
     t_copy(col, 1, p_dev).wait_send()
     t_copy(xcol, 2, p_dev).wait_send()
+    g_copy(GROUPS).wait_send()
 
     give(GROUPS - 1).start()
     keep = pltpu.make_async_copy(
@@ -288,19 +338,20 @@
             out_specs=any_spec,
             scratch_shapes=[
                 pltpu.VMEM((8, BLOCKS * RB, 128), F32),
-                pltpu.VMEM((4, GROUPS * PW, 128), F32),
+                pltpu.VMEM((4, GROUPS * PW, 2 * PW), F32),
                 pltpu.VMEM((2, ROWS, COLS), F32),
-                pltpu.VMEM((HW, COLS), F32),
-                pltpu.VMEM((HW, COLS), F32),
-                pltpu.VMEM((HW, HW), F32),
-                pltpu.VMEM((HW, HW), F32),
-                pltpu.VMEM((HW, HW), F32),
                 pltpu.VMEM((GW, COLS), F32),
+                pltpu.VMEM((3, HW, HW), F32),
+                pltpu.VMEM((2, 3, HW, HW), F32),
+                pltpu.VMEM((3, HW, HW), F32),
+                pltpu.VMEM((3, GW, COLS), BF16),
                 pltpu.SemaphoreType.DMA((GROUPS,)),
                 pltpu.SemaphoreType.DMA((3,)),
                 pltpu.SemaphoreType.DMA((3,)),
                 pltpu.SemaphoreType.DMA((8, BLOCKS)),
                 pltpu.SemaphoreType.DMA((8, BLOCKS)),
+                pltpu.SemaphoreType.DMA,
+                pltpu.SemaphoreType.DMA((2,)),
                 pltpu.SemaphoreType.DMA((GROUPS,)),
                 pltpu.SemaphoreType.DMA((GROUPS,)),
                 pltpu.SemaphoreType.DMA((3,)),

time: 272 us -> 237 us (0.87)
  Pallas kernels: 264 us -> 230 us
    pallas_call x1, Pallas kernels: 264 us -> 230 us  [local_apply(): pl.pallas_call(kernel, out_shape=jax.ShapeDtypeStruct((ROWS, 2 * COLS), F...]
where the time goes in v2:
time: 237 us
  Pallas kernels  230 us (97%)
  local copies, waits for them, and re-layouts  7.11 us (3%)
    pallas_call x1, Pallas kernels, local_apply(): pl.pallas_call(kernel, out_shape=jax.ShapeDtypeStruct((ROWS, 2 * COLS), F...  230 us

profile of v2, /device:TPU:0, one launch (start us, length us, event | category | flops | bytes accessed | tf_op | source)
XLA Modules:
  0.0 237.1 jit_solution(1018563981443264049)
XLA Ops:
  0.0 1.4 copy.6
  1.5 1.0 reshape.10.t_hbm
  2.5 230.0 %panels.1 = f32[2048,512]{1,0:T(8,128)} custom-call(f32[2048,1024]{1,0:T(8,128)} %v_hbm.1, f32[512,128]{1,0:T(8,128)} %reshape.10.t_hbm, f32[2,2048,256]{2,1,0:T(8,128)} %bitcast.5), custom_call_target="tpu_custom_call" | custom-call | tf_op jit(solution)/shard_map/panels/pallas_call | solution.py:334
  232.4 4.6 %copy.8 = f32[2048,512]{1,0:T(8,128)} copy(f32[2048,512]{1,0:T(8,128)} %panels.1) | data formatting | bytes 8388608

commit v3 on v2

--- a/solution.py
+++ b/solution.py
@@ -12,9 +12,16 @@
 RB = 256
 GROUPS = 8
 BLOCKS = GROUPS * (GROUPS + 1) // 2
-HALF = RB // 2
+PACK = 64
+STARTS = [n * (n - 1) // 2 for n in range(1, GROUPS + 1)]
+Y_ROWS = 128
+Y_PACKED = 96
+X_ONLY = 28
+LAST_GIVES = 2
+SPAN = 2 * RB
 AHEAD_W = 5
-OWN_LEAD = 4
+X_LEAD = 4
+Y_LEAD = 6
 COLS = 256
 ROWS = 2048
 GW = GROUPS * PW
@@ -44,8 +51,9 @@
     return dot6(split3(a), split3(b))
 
 
-def kernel(v_hbm, t_hbm, z_hbm, out_hbm, v_buf, t_buf, x_buf, w_buf, g_part, g_in, g_last, y_buf,
-           loc_sem, t_send, t_recv, send, recv, g_send, g_recv, c_send, c_recv, io_sem):
+def kernel(v_hbm, t_hbm, z_hbm, out_hbm, v_buf, t_own, t_buf, x_buf, w_buf, g_part, g_in, g_last, y_buf,
+           xb_buf, y_out, y_in, yb_buf, loc_sem, t_send, t_recv, send, recv, g_send, g_recv, c_send, c_recv,
+           y_send, y_recv, o_sem, io_sem):
     row = lax.axis_index('row')
     col = lax.axis_index('col')
     orow = 1 - row
@@ -59,7 +67,7 @@
     ds = orow * 4 + xcol
 
     def vmem(slot, blk, off=0, size=RB):
-        return v_buf.at[slot, pl.ds(pl.multiple_of(blk * RB + off, HALF), size), :]
+        return v_buf.at[slot, pl.ds(pl.multiple_of(blk * RB + off, 8), size), :]
 
     def rcopy(slot, blk, kind, dev, off=0, size=RB):
         return pltpu.make_async_remote_copy(
@@ -68,15 +76,61 @@
 
     OX, OY, OP, FX, FY, PX, PY, PD = range(8)
 
-    def own(blk):
-        return (rcopy(me, blk, OX, x_dev), rcopy(me, blk, OY, y_dev), rcopy(me, blk, OP, p_dev))
-
-    def fwd(blk):
-        return (rcopy(xs, blk, FY, y_dev, 0, HALF), rcopy(ys, blk, FX, x_dev, HALF, HALF),
-                rcopy(xs, blk, PX, p_dev), rcopy(ys, blk, PY, p_dev))
-
-    def diag(blk):
-        return rcopy(ds, blk, PD, p_dev)
+    def folded(blk):
+        found = blk == STARTS[0]
+        for b in STARTS[1:]:
+            found = jnp.logical_or(found, blk == b)
+        return found
+
+    def whole(slot, blk, kind, dev, act):
+        if isinstance(blk, int):
+            off = PACK if blk in STARTS else 0
+            act(rcopy(slot, blk, kind, dev, off, RB - off))
+            return
+        fold = folded(blk)
+
+        @pl.when(fold)
+        def _():
+            act(rcopy(slot, blk, kind, dev, PACK, RB - PACK))
+
+        @pl.when(jnp.logical_not(fold))
+        def _():
+            act(rcopy(slot, blk, kind, dev))
+
+    def own_x(blk, act):
+        whole(me, blk, OX, x_dev, act)
+        whole(me, blk, OP, p_dev, act)
+
+    def own_y(blk, act):
+        whole(me, blk, OY, y_dev, act)
+
+    def mates(blk, act):
+        whole(xs, blk, PX, p_dev, act)
+        whole(ys, blk, PY, p_dev, act)
+
+    def cross(blk, ys_slot, xs_slot, act):
+        fold = folded(blk)
+
+        @pl.when(jnp.logical_and(blk < X_ONLY, fold))
+        def _():
+            act(rcopy(xs_slot, blk, FY, y_dev, PACK, Y_PACKED))
+            act(rcopy(ys_slot, blk, FX, x_dev, PACK + Y_PACKED, RB - PACK - Y_PACKED))
+
+        @pl.when(jnp.logical_and(blk < X_ONLY, jnp.logical_not(fold)))
+        def _():
+            act(rcopy(xs_slot, blk, FY, y_dev, 0, Y_ROWS))
+            act(rcopy(ys_slot, blk, FX, x_dev, Y_ROWS, RB - Y_ROWS))
+
+        @pl.when(blk >= X_ONLY)
+        def _():
+            whole(ys_slot, blk, FX, x_dev, act)
+
+    def diag(blk, act):
+        whole(ds, blk, PD, p_dev, act)
+
+    start = lambda c: c.start()
+    sent_out = lambda c: c.wait_send()
+    landed = lambda c: c.wait_recv()
 
     def t_copy(slot, kind, dev):
         return pltpu.make_async_remote_copy(
@@ -90,39 +144,62 @@
             v_hbm.at[pl.ds(RB * k, RB * n), pl.ds(2 * PW * k, 2 * PW)],
             v_buf.at[me, pl.ds(RB * o, RB * n), :], loc_sem.at[n - 1])
 
-    for n in range(1, GROUPS + 1):
+    t_in = pltpu.make_async_copy(t_hbm, t_own, io_sem.at[0])
+    z_in = pltpu.make_async_copy(z_hbm, x_buf, io_sem.at[1])
+    soon = 4
+    t_in.start()
+    for n in range(1, soon + 1):
         local_v(n).start()
-    t_in = pltpu.make_async_copy(t_hbm, t_buf.at[col], io_sem.at[0])
-    t_in.start()
-    z_in = pltpu.make_async_copy(z_hbm, x_buf, io_sem.at[1])
-    z_in.start()
 
     barrier = pltpu.get_barrier_semaphore()
     for dev in (x_dev, y_dev, p_dev):
         pl.semaphore_signal(barrier, inc=1, device_id=dev, device_id_type=MESH)
+    t_in.wait()
+    for k in range(GROUPS):
+        t_buf[col, k * PW:(k + 1) * PW, :] = jnp.concatenate(
+            [t_own[2 * k * PW:(2 * k + 1) * PW, :], t_own[(2 * k + 1) * PW:(2 * k + 2) * PW, :]], axis=1)
+    half_lane = lax.broadcasted_iota(jnp.int32, (PW, 128), 1) < PW
+
+    def fold_own(n):
+        r = RB * STARTS[n - 1]
+        low = v_buf[me, r:r + PW, :]
+        high = v_buf[me, r + PW:r + 2 * PW, :]
+        v_buf[me, r + PW:r + 2 * PW, :] = jnp.where(half_lane, low, pltpu.roll(high, PW, 1))
+
+    for n in range(1, soon + 1):
+        local_v(n).wait()
+        fold_own(n)
+    for m in range(soon + 1, GROUPS + 1):
+        local_v(m).start()
+    z_in.start()
     pl.semaphore_wait(barrier, 3)
 
-    for n in range(1, GROUPS + 1):
-        local_v(n).wait()
-        if n == 4:
-            for b in range(OWN_LEAD):
-                for c in own(b):
-                    c.start()
-            t_in.wait()
+    for b in range(max(X_LEAD, Y_LEAD)):
+        if b < X_LEAD:
+            own_x(b, start)
+        if b < Y_LEAD:
+            own_y(b, start)
+        if b == 1:
             t_copy(col, 0, x_dev).start()
             t_copy(col, 1, p_dev).start()
+    for m in range(soon + 1, GROUPS + 1):
+        local_v(m).wait()
+        fold_own(m)
     z_in.wait()
 
     def pump(blk, _):
-        rcopy(xs, blk, OX, x_dev).wait_recv()
-        rcopy(ys, blk, OY, y_dev).wait_recv()
-        for c in fwd(blk):
-            c.start()
-
-        @pl.when(blk + OWN_LEAD < BLOCKS)
-        def _():
-            for c in own(blk + OWN_LEAD):
-                c.start()
+        whole(xs, blk, OX, x_dev, landed)
+        whole(ys, blk, OY, y_dev, landed)
+        cross(blk, ys, xs, start)
+        mates(blk, start)
+
+        @pl.when(blk + X_LEAD < BLOCKS)
+        def _():
+            own_x(blk + X_LEAD, start)
+
+        @pl.when(blk + Y_LEAD < BLOCKS)
+        def _():
+            own_y(blk + Y_LEAD, start)
         return 0
 
     def pump_to(done, target):
@@ -131,20 +208,23 @@
         return target
 
     def take_diag(blk):
-        rcopy(ds, blk, FY, y_dev, 0, HALF).wait_recv()
-        rcopy(ds, blk, FX, x_dev, HALF, HALF).wait_recv()
-        diag(blk).start()
+        cross(blk, ds, ds, landed)
+        diag(blk, start)
 
     def need(blk):
-        rcopy(me, blk, OP, p_dev).wait_recv()
-        rcopy(me, blk, PX, p_dev).wait_recv()
-        rcopy(me, blk, PY, p_dev).wait_recv()
-        rcopy(me, blk, PD, p_dev).wait_recv()
-
-    def rows_of(blk, dds):
+        for kind in (OP, PX, PY, PD):
+            whole(me, blk, kind, p_dev, landed)
+
+    def unfold(t, fold):
+        p = t[PW:2 * PW]
+        top = jnp.concatenate(
+            [jnp.where(half_lane, p, 0.0), jnp.where(half_lane, pltpu.roll(p, PW, 1), 0.0)], axis=0)
+        return jnp.concatenate([jnp.where(fold, top, t[:2 * PW]), t[2 * PW:]], axis=0)
+
+    def rows_of(blk, dds, fold):
         r = pl.ds(pl.multiple_of(blk * RB, RB), RB)
         return jnp.concatenate(
-            [jnp.concatenate([v_buf[dd * 4 + e, r, :] for e in range(4)], axis=1) for dd in dds], axis=0)
+            [jnp.concatenate([unfold(v_buf[dd * 4 + e, r, :], fold) for e in range(4)], axis=1) for dd in dds], axis=0)
 
     def gram(cols, vals):
         first = [t[:HW] for t in cols]
@@ -225,7 +305,7 @@
 
         def load(i):
             r = pl.ds(pl.multiple_of((k + i) * RB, RB), RB)
-            v = split3(rows_of(first + i, (core, 1 - core)))
+            v = split3(rows_of(first + i, (core, 1 - core), i == 0))
             x = split3(jnp.concatenate([x_buf[core, r, :], x_buf[1 - core, r, :]], axis=0))
             t = [p.T for p in v]
             w_buf[...] += dot6(t, x)
@@ -271,6 +351,11 @@
                   for par in range(2)]
         y1 = dot_f32(ts[1], w1)
         y0 = dot_f32(ts[0], w0 - dot_f32(g01, y1))
+        @pl.when(k == 0)
+        def _():
+            for e in range(4):
+                for par, y in enumerate((y0, y1)):
+                    y_out[e * 128 + par * PW:e * 128 + (par + 1) * PW, :] = y[e * PW:(e + 1) * PW]
         for e in range(4):
             for par, y in enumerate((y0, y1)):
                 for q, part in enumerate(split3(y[e * PW:(e + 1) * PW])):
@@ -280,33 +365,83 @@
             blk = first + i
             pumped = pump_to(pumped, first + n - 1 + AHEAD_W + (i + 1) // 2)
             rx = pl.ds(pl.multiple_of((k + i) * RB, RB), RB)
-            delta = dot6(split3(rows_of(blk, (0, 1))), [y_buf[q] for q in range(3)])
+            delta = dot6(split3(rows_of(blk, (0, 1), i == 0)), [y_buf[q] for q in range(3)])
             x_buf[0, rx, :] = x_buf[0, rx, :] - delta[:RB]
             x_buf[1, rx, :] = x_buf[1, rx, :] - delta[RB:]
 
-            @pl.when(jnp.logical_and(k == 0, i > 0))
+            @pl.when(jnp.logical_and(k == 1, i < GROUPS - LAST_GIVES))
             def _():
-                give(i - 1).start()
+                give(i).start()
             return pumped
 
-        pumped = lax.fori_loop(0, n, update_step, pumped)
+        pumped = lax.fori_loop(0, jnp.where(k == 0, 0, n), update_step, pumped)
         return pumped, diag_done
 
     def give(i):
         r = pl.ds(pl.multiple_of(i * RB, RB), RB)
         return pltpu.make_async_remote_copy(
-            src_ref=x_buf.at[orow, r, :],
-            dst_ref=out_hbm.at[r, pl.ds(pl.multiple_of(row * COLS, COLS), COLS)],
-            send_sem=c_send.at[i], recv_sem=c_recv.at[i], device_id=y_dev, device_id_type=MESH)
+            src_ref=x_buf.at[orow, r, :], dst_ref=xb_buf.at[r, :], send_sem=c_send.at[i], recv_sem=c_recv.at[i],
+            device_id=y_dev, device_id_type=MESH)
+
+    y_copy = pltpu.make_async_remote_copy(
+        src_ref=y_out, dst_ref=y_in, send_sem=y_send, recv_sem=y_recv, device_id=y_dev, device_id_type=MESH)
 
     lax.fori_loop(0, GROUPS, group, (0, 0))
 
+    first_last = BLOCKS - GROUPS
+
+    def span_of(i):
+        return pl.ds(pl.multiple_of(i * SPAN, SPAN), SPAN)
+
+    def v_span(i):
+        r = pl.ds(pl.multiple_of(first_last * RB + i * SPAN, SPAN), SPAN)
+        return split3(jnp.concatenate([unfold(v_buf[row * 4 + e, r, :], i == 0) for e in range(4)], axis=1))
+
+    def put(i, side):
+        at = row if side == 0 else orow
+        src = x_buf.at[row, span_of(i), :] if side == 0 else xb_buf.at[span_of(i), :]
+        return pltpu.make_async_copy(
+            src, out_hbm.at[span_of(i), pl.ds(pl.multiple_of(at * COLS, COLS), COLS)], o_sem.at[side, i])
+
+    spans = ROWS // SPAN
+
+    def mine(i, _):
+        x_buf[row, span_of(i), :] = x_buf[row, span_of(i), :] - dot6(v_span(i), [y_buf[q] for q in range(3)])
+
+        @pl.when(i == 0)
+        def _():
+            y_copy.start()
+            for g in range(GROUPS - LAST_GIVES, GROUPS):
+                give(g).start()
+
+        @pl.when(i > 0)
+        def _():
+            put(i - 1, 0).start()
+        return 0
+    lax.fori_loop(0, spans, mine, 0)
+
+    y_copy.wait_recv()
+    for q, part in enumerate(split3(y_in[...])):
+        yb_buf[q] = part
+    put(spans - 1, 0).start()
+
+    def theirs(i, _):
+        for h in range(SPAN // RB):
+            give(i * (SPAN // RB) + h).wait_recv()
+        xb_buf[span_of(i), :] = xb_buf[span_of(i), :] - dot6(v_span(i), [yb_buf[q] for q in range(3)])
+
+        @pl.when(i > 0)
+        def _():
+            put(i - 1, 1).start()
+        return 0
+    lax.fori_loop(0, spans, theirs, 0)
+
     def drain(blk, _):
-        for c in own(blk):
-            c.wait_send()
-        for c in fwd(blk):
-            c.wait_send()
-        diag(blk).wait_send()
+        own_x(blk, sent_out)
+        own_y(blk, sent_out)
+        cross(blk, ys, xs, sent_out)
+        mates(blk, sent_out)
+        diag(blk, sent_out)
         return 0
     lax.fori_loop(0, BLOCKS, drain, 0)
     t_copy(col, 0, x_dev).wait_send()
@@ -314,21 +449,22 @@
     t_copy(xcol, 2, p_dev).wait_send()
     g_copy(GROUPS).wait_send()
 
-    give(GROUPS - 1).start()
-    keep = pltpu.make_async_copy(
-        x_buf.at[row], out_hbm.at[:, pl.ds(pl.multiple_of(row * COLS, COLS), COLS)], io_sem.at[2])
-    keep.start()
-    keep.wait()
+
+    put(spans - 1, 1).start()
+    y_copy.wait_send()
 
     def drain_c(i, _):
-        give(i).wait()
+        give(i).wait_send()
         return 0
     lax.fori_loop(0, GROUPS, drain_c, 0)
+    for i in range(spans):
+        put(i, 0).wait()
+        put(i, 1).wait()
 
 
 def solution(mesh):
     def local_apply(v_loc, t_loc, z_loc):
-        t_pk = t_loc.reshape(GROUPS, 2, PW, PW).transpose(0, 2, 1, 3).reshape(GROUPS * PW, 2 * PW)
+        t_pk = t_loc.reshape(2 * GROUPS * PW, PW)
         z_pk = z_loc.reshape(2, ROWS, COLS)
         any_spec = pl.BlockSpec(memory_space=pl.ANY)
         return pl.pallas_call(
@@ -338,12 +474,17 @@
             out_specs=any_spec,
             scratch_shapes=[
                 pltpu.VMEM((8, BLOCKS * RB, 128), F32),
+                pltpu.VMEM((2 * GROUPS * PW, PW), F32),
                 pltpu.VMEM((4, GROUPS * PW, 2 * PW), F32),
                 pltpu.VMEM((2, ROWS, COLS), F32),
                 pltpu.VMEM((GW, COLS), F32),
                 pltpu.VMEM((3, HW, HW), F32),
                 pltpu.VMEM((2, 3, HW, HW), F32),
                 pltpu.VMEM((3, HW, HW), F32),
+                pltpu.VMEM((3, GW, COLS), BF16),
+                pltpu.VMEM((ROWS, COLS), F32),
+                pltpu.VMEM((GW, COLS), F32),
+                pltpu.VMEM((GW, COLS), F32),
                 pltpu.VMEM((3, GW, COLS), BF16),
                 pltpu.SemaphoreType.DMA((GROUPS,)),
                 pltpu.SemaphoreType.DMA((3,)),
@@ -354,7 +495,10 @@
                 pltpu.SemaphoreType.DMA((2,)),
                 pltpu.SemaphoreType.DMA((GROUPS,)),
                 pltpu.SemaphoreType.DMA((GROUPS,)),
-                pltpu.SemaphoreType.DMA((3,)),
+                pltpu.SemaphoreType.DMA,
+                pltpu.SemaphoreType.DMA,
+                pltpu.SemaphoreType.DMA((2, ROWS // SPAN)),
+                pltpu.SemaphoreType.DMA((2,)),
             ],
             compiler_params=pltpu.CompilerParams(
                 collective_id=0, has_side_effects=True, vmem_limit_bytes=VMEM_LIMIT),

time: 237 us -> 215 us (0.907)
  Pallas kernels: 230 us -> 210 us
  local copies, waits for them, and re-layouts: 7.11 us -> 4.64 us
    pallas_call x1, Pallas kernels: 230 us -> 210 us  [local_apply(): pl.pallas_call(kernel, out_shape=jax.ShapeDtypeStruct((ROWS, 2 * COLS), F...]
    reshape x2 -> x0, local copies, waits for them, and re-layouts: 2.46 us -> none  [local_apply(): t_loc.reshape(GROUPS, 2, PW, PW).transpose(0, 2, 1, 3)]
where the time goes in v3:
time: 215 us
  Pallas kernels  210 us (98%)
  local copies, waits for them, and re-layouts  4.64 us (2%)
    pallas_call x1, Pallas kernels, local_apply(): pl.pallas_call(kernel, out_shape=jax.ShapeDtypeStruct((ROWS, 2 * COLS), F...  210 us
    unnamed x1, local copies, waits for them, and re-layouts  4.64 us

profile of v3, /device:TPU:0, one launch (start us, length us, event | category | flops | bytes accessed | tf_op | source)
XLA Modules:
  0.0 214.8 jit_solution(814190661163356770)
XLA Ops:
  0.0 210.1 %panels.1 = f32[2048,512]{1,0:T(8,128)} custom-call(f32[2048,1024]{1,0:T(8,128)} %v_hbm.1, f32[1024,64]{1,0:T(8,128)} %bitcast.3, f32[2,2048,256]{2,1,0:T(8,128)} %bitcast.2), custom_call_target="tpu_custom_call" | custom-call | tf_op jit(solution)/shard_map/panels/pallas_call | solution.py:470
  210.1 4.6 %copy.5 = f32[2048,512]{1,0:T(8,128)} copy(f32[2048,512]{1,0:T(8,128)} %panels.1) | data formatting | bytes 8388608

commit v4 on v3

--- a/solution.py
+++ b/solution.py
@@ -16,7 +16,7 @@
 STARTS = [n * (n - 1) // 2 for n in range(1, GROUPS + 1)]
 Y_ROWS = 128
 Y_PACKED = 96
-X_ONLY = 28
+X_ONLY = 30
 LAST_GIVES = 2
 SPAN = 2 * RB
 AHEAD_W = 5
@@ -26,7 +26,7 @@
 ROWS = 2048
 GW = GROUPS * PW
 HW = GW // 2
-VMEM_LIMIT = 66 * 10**6
+VMEM_LIMIT = 60 * 10**6
 
 
 def split3(x):
@@ -51,9 +51,9 @@
     return dot6(split3(a), split3(b))
 
 
-def kernel(v_hbm, t_hbm, z_hbm, out_hbm, v_buf, t_own, t_buf, x_buf, w_buf, g_part, g_in, g_last, y_buf,
+def kernel(v_hbm, t_hbm, z_hbm, out_ref, v_buf, t_own, t_buf, x_buf, w_buf, g_part, g_in, g_last, y_buf,
            xb_buf, y_out, y_in, yb_buf, loc_sem, t_send, t_recv, send, recv, g_send, g_recv, c_send, c_recv,
-           y_send, y_recv, o_sem, io_sem):
+           y_send, y_recv, io_sem):
     row = lax.axis_index('row')
     col = lax.axis_index('col')
     orow = 1 - row
@@ -290,10 +290,11 @@
             g_copy(n - 1).wait_send()
         g_part[...] = jnp.zeros_like(g_part)
 
-        def arrive(i, carry):
+        def arrive(i, carry, pumping=True):
             pumped, diag_done = carry
             blk = first + i
-            pumped = pump_to(pumped, blk + AHEAD_W)
+            if pumping:
+                pumped = pump_to(pumped, blk + AHEAD_W)
 
             def dg(b, _):
                 take_diag(b)
@@ -312,12 +313,13 @@
             return v, t
 
         def gather_step(i, carry):
-            carry = arrive(i, carry)
+            carry = arrive(i, carry, False)
             v, t = load(i)
             gs = gram([p[:, :RB] for p in t], [p[:RB] for p in v])
             for q in range(3):
                 g_part[q] += gs[q]
-            return carry
+            pumped, diag_done = carry
+            return pump_to(pumped, first + i + 1 + AHEAD_W), diag_done
 
         carry = lax.fori_loop(0, step, gather_step, (pumped, diag_done))
         pumped, diag_done = arrive(step, carry)
@@ -397,42 +399,30 @@
         r = pl.ds(pl.multiple_of(first_last * RB + i * SPAN, SPAN), SPAN)
         return split3(jnp.concatenate([unfold(v_buf[row * 4 + e, r, :], i == 0) for e in range(4)], axis=1))
 
-    def put(i, side):
-        at = row if side == 0 else orow
-        src = x_buf.at[row, span_of(i), :] if side == 0 else xb_buf.at[span_of(i), :]
-        return pltpu.make_async_copy(
-            src, out_hbm.at[span_of(i), pl.ds(pl.multiple_of(at * COLS, COLS), COLS)], o_sem.at[side, i])
+    def half_of(i, at):
+        return out_ref.at[span_of(i), pl.ds(pl.multiple_of(at * COLS, COLS), COLS)]
 
     spans = ROWS // SPAN
 
     def mine(i, _):
-        x_buf[row, span_of(i), :] = x_buf[row, span_of(i), :] - dot6(v_span(i), [y_buf[q] for q in range(3)])
+        half_of(i, row)[...] = x_buf[row, span_of(i), :] - dot6(v_span(i), [y_buf[q] for q in range(3)])
 
         @pl.when(i == 0)
         def _():
             y_copy.start()
             for g in range(GROUPS - LAST_GIVES, GROUPS):
                 give(g).start()
-
-        @pl.when(i > 0)
-        def _():
-            put(i - 1, 0).start()
         return 0
     lax.fori_loop(0, spans, mine, 0)
 
     y_copy.wait_recv()
     for q, part in enumerate(split3(y_in[...])):
         yb_buf[q] = part
-    put(spans - 1, 0).start()
 
     def theirs(i, _):
         for h in range(SPAN // RB):
             give(i * (SPAN // RB) + h).wait_recv()
-        xb_buf[span_of(i), :] = xb_buf[span_of(i), :] - dot6(v_span(i), [yb_buf[q] for q in range(3)])
-
-        @pl.when(i > 0)
-        def _():
-            put(i - 1, 1).start()
+        half_of(i, orow)[...] = xb_buf[span_of(i), :] - dot6(v_span(i), [yb_buf[q] for q in range(3)])
         return 0
     lax.fori_loop(0, spans, theirs, 0)
 
@@ -450,16 +440,12 @@
     g_copy(GROUPS).wait_send()
 
 
-    put(spans - 1, 1).start()
     y_copy.wait_send()
 
     def drain_c(i, _):
         give(i).wait_send()
         return 0
     lax.fori_loop(0, GROUPS, drain_c, 0)
-    for i in range(spans):
-        put(i, 0).wait()
-        put(i, 1).wait()
 
 
 def solution(mesh):
@@ -469,9 +455,9 @@
         any_spec = pl.BlockSpec(memory_space=pl.ANY)
         return pl.pallas_call(
             kernel,
-            out_shape=jax.ShapeDtypeStruct((ROWS, 2 * COLS), F32),
+            out_shape=pltpu.VMEM((ROWS, 2 * COLS), F32),
             in_specs=[any_spec] * 3,
-            out_specs=any_spec,
+            out_specs=pl.BlockSpec(memory_space=pltpu.VMEM),
             scratch_shapes=[
                 pltpu.VMEM((8, BLOCKS * RB, 128), F32),
                 pltpu.VMEM((2 * GROUPS * PW, PW), F32),
@@ -497,7 +483,6 @@
                 pltpu.SemaphoreType.DMA((GROUPS,)),
                 pltpu.SemaphoreType.DMA,
                 pltpu.SemaphoreType.DMA,
-                pltpu.SemaphoreType.DMA((2, ROWS // SPAN)),
                 pltpu.SemaphoreType.DMA((2,)),
             ],
             compiler_params=pltpu.CompilerParams(

time: 215 us -> 211 us (0.981)
  local copies, waits for them, and re-layouts: 4.64 us -> 2.02 us
    unnamed x1, local copies, waits for them, and re-layouts: 4.64 us -> 2.02 us
where the time goes in v4:
time: 211 us
  Pallas kernels  209 us (99%)
    pallas_call x1, Pallas kernels, local_apply(): pl.pallas_call(kernel, out_shape=pltpu.VMEM((ROWS, 2 * COLS), F32), in_sp...  209 us

profile of v4, /device:TPU:0, one launch (start us, length us, event | category | flops | bytes accessed | tf_op | source)
XLA Modules:
  0.0 210.9 jit_solution(17101066506525034195)
XLA Ops:
  0.0 208.8 %panels.1 = f32[2048,512]{1,0:T(8,128)S(1)} custom-call(f32[2048,1024]{1,0:T(8,128)} %v_hbm.1, f32[1024,64]{1,0:T(8,128)} %bitcast.3, f32[2,2048,256]{2,1,0:T(8,128)} %bitcast.2), custom_call_target="tpu_custom_call" | custom-call | tf_op jit(solution)/shard_map/panels/pallas_call | solution.py:456
  208.9 2.0 copy.5

commit v5 on v4

--- a/solution.py
+++ b/solution.py
@@ -18,7 +18,7 @@
 Y_PACKED = 96
 X_ONLY = 30
 LAST_GIVES = 2
-SPAN = 2 * RB
+SPAN = RB
 AHEAD_W = 5
 X_LEAD = 4
 Y_LEAD = 6

time: 211 us -> 211 us (level)
  no operation moved by 1% of the time
where the time goes in v5:
time: 211 us
  Pallas kernels  208 us (99%)
    pallas_call x1, Pallas kernels, local_apply(): pl.pallas_call(kernel, out_shape=pltpu.VMEM((ROWS, 2 * COLS), F32), in_sp...  208 us

profile of v5, /device:TPU:0, one launch (start us, length us, event | category | flops | bytes accessed | tf_op | source)
XLA Modules:
  0.0 210.5 jit_solution(8231253938251246443)
XLA Ops:
  0.0 208.5 %panels.1 = f32[2048,512]{1,0:T(8,128)S(1)} custom-call(f32[2048,1024]{1,0:T(8,128)} %v_hbm.1, f32[1024,64]{1,0:T(8,128)} %bitcast.3, f32[2,2048,256]{2,1,0:T(8,128)} %bitcast.2), custom_call_target="tpu_custom_call" | custom-call | tf_op jit(solution)/shard_map/panels/pallas_call | solution.py:456
  208.5 2.0 copy.5

commit v6 on v5

--- a/solution.py
+++ b/solution.py
@@ -179,7 +179,7 @@
             own_x(b, start)
         if b < Y_LEAD:
             own_y(b, start)
-        if b == 1:
+        if b == 3:
             t_copy(col, 0, x_dev).start()
             t_copy(col, 1, p_dev).start()
     for m in range(soon + 1, GROUPS + 1):

time: 211 us -> 211 us (level)
  no operation moved by 1% of the time
where the time goes in v6:
time: 211 us
  Pallas kernels  208 us (99%)
    pallas_call x1, Pallas kernels, local_apply(): pl.pallas_call(kernel, out_shape=pltpu.VMEM((ROWS, 2 * COLS), F32), in_sp...  208 us

profile of v6, /device:TPU:0, one launch (start us, length us, event | category | flops | bytes accessed | tf_op | source)
XLA Modules:
  0.0 210.5 jit_solution(13316167445666266656)
XLA Ops:
  0.0 208.5 %panels.1 = f32[2048,512]{1,0:T(8,128)S(1)} custom-call(f32[2048,1024]{1,0:T(8,128)} %v_hbm.1, f32[1024,64]{1,0:T(8,128)} %bitcast.3, f32[2,2048,256]{2,1,0:T(8,128)} %bitcast.2), custom_call_target="tpu_custom_call" | custom-call | tf_op jit(solution)/shard_map/panels/pallas_call | solution.py:456
  208.5 2.0 copy.5
